TPU v7x, 32 devices: a whole 2x2x4 slice. The times are simulated.
32 devices in a mesh: grp: 8 (over y, x, core), cube: 4 (over z).
Axes of the slice: x: 2, y: 2, z: 4, core: 2. Of those that a mesh axis runs over, the one named last changes fastest.
Arguments:
- params: float32 [8, 4, 4096, 128], P('grp', 'cube'), may hold values from -8 to 8
- estimate: float32 [8, 4, 4096, 128], P('grp', 'cube'), may hold values from -6 to 6
- neighbour_sum: float32 [8, 4, 4096, 128], P('grp', 'cube'), may hold values from -10 to 10
- gradient: bfloat16 [8, 4, 4096, 128], P('grp', 'cube'), may hold values from -6 to 6
- block_ids: int32 [8, 4, 128], P('grp', 'cube'), may hold values from 0 to 4095, as said below
Outputs:
- new_params: float32 [8, 4, 4096, 128], P('grp', 'cube')
- new_estimate: float32 [8, 4, 4096, 128], P('grp', 'cube')
- new_neighbour_sum: float32 [8, 4, 4096, 128], P('grp', 'cube')
- consensus: float32 [1], replicated
Inputs may be any that keep to these rules, and one draw needn't show every extreme that they name: `block_ids`: each replica's row holds 128 distinct block numbers in ascending order.
All inputs are finite; a program needn't handle non-finite values.
Results may differ from a plain program's by a relative error of at most 0.003.
Values may be sent and summed in bfloat16 or wider, within the bound.
A program may use at most 64 MiB of HBM per device.

v0:
```python
import jax
import jax.numpy as jnp
from jax import lax
from jax.sharding import PartitionSpec as P

LEARN_RATE = 0.1
INNER_RATE = 0.6
OUTER_RATE = 0.5


def partner(block, axis, stride):
    count = lax.axis_size(axis)
    route = []
    for low in range(count):
        high = low | 1 << stride
        if high != low and high < count:
            route += [(low, high), (high, low)]
    return lax.ppermute(block, axis, route)


def local(params, estimate, neighbour_sum, gradient, block_ids):
    weights_now = params[0, 0]
    current = estimate[0, 0]
    chosen = block_ids[0, 0]
    stepped = weights_now - LEARN_RATE * gradient[0, 0].astype(jnp.float32)
    picked = (stepped[chosen] - current[chosen]).astype(jnp.bfloat16)
    new_estimate = current.at[chosen].add(picked.astype(jnp.float32))
    summed = neighbour_sum[0, 0]
    cube_count = lax.axis_size("cube")
    cube_bits = cube_count.bit_length() - 1
    for level in range(cube_bits):
        their_values, their_rows = partner((picked, chosen), "cube", level)
        summed = summed.at[their_rows].add(their_values.astype(jnp.float32))
    mixed_in = stepped + INNER_RATE * (summed - cube_bits * new_estimate) / (cube_bits + 1)
    group_count = lax.axis_size("grp")
    group_bits = group_count.bit_length() - 1
    group_mean = (
        lax.psum_scatter(
            mixed_in.astype(jnp.bfloat16), "cube", scatter_dimension=0, tiled=True
        ).astype(jnp.float32)
        / cube_count
    )
    combined = group_mean
    for level in range(group_bits):
        combined = combined + partner(group_mean.astype(jnp.bfloat16), "grp", level).astype(
            group_mean.dtype
        )
    shortfall = combined / (group_bits + 1) - group_mean
    spread_sum = lax.psum(jnp.sum(shortfall * shortfall), ("grp", "cube"))
    correction = lax.all_gather(shortfall.astype(jnp.bfloat16), "cube", axis=0, tiled=True).astype(
        shortfall.dtype
    )
    new_params = mixed_in + OUTER_RATE * correction
    entries = weights_now.shape[0] * weights_now.shape[1]
    consensus = jnp.sqrt(spread_sum / (group_count * entries)).reshape(1)
    return (new_params[None, None], new_estimate[None, None], summed[None, None], consensus)


def solution(mesh):
    in_specs = (
        P("grp", "cube", None, None),
        P("grp", "cube", None, None),
        P("grp", "cube", None, None),
        P("grp", "cube", None, None),
        P("grp", "cube", None),
    )
    out_specs = (
        P("grp", "cube", None, None),
        P("grp", "cube", None, None),
        P("grp", "cube", None, None),
        P(),
    )
    return jax.shard_map(local, mesh=mesh, in_specs=in_specs, out_specs=out_specs, check_vma=False)
```

profile of v0, /device:TPU:0, one launch (start us, length us, event | category | flops | bytes accessed | tf_op | source)
XLA Modules:
  0.0 131.0 jit_solution(15769571404673725755)
XLA Ops:
  7.2 0.0 copy-start
  7.2 0.0 reduce-scatter.2.cloned.1.call-start
  7.2 3.2 %copy.14 = f32[1,1,4096,128]{3,2,1,0:T(8,128)} copy(f32[1,1,4096,128]{3,2,1,0:T(8,128)} %param.6) | data formatting | bytes 4194304
  10.4 0.0 copy-done
  10.4 0.0 copy-start.3
  10.4 0.0 copy-start.1
  10.4 0.0 copy-start.2
  10.4 1.3 %copy.15 = f32[1,1,4096,128]{3,2,1,0:T(8,128)} copy(f32[1,1,4096,128]{3,2,1,0:T(8,128)S(1)} %copy-done) | data formatting | bytes 4194304
  11.7 0.0 copy-done.3
  11.7 4.1 %collective-permute-start.2 = (s32[128]{0:T(128)S(1)}, s32[128]{0:T(128)S(1)}, u32[]{:S(2)}, u32[]{:S(2)}) collective-permute-start(s32[128]{0:T(128)S(1)} %bitcast.19), channel_id=1, source_target_pairs={{0,2},{2,0},{1,3},{3,1},{4,6},{6,4},{5,7},{7,5},{8,10},{10,8},{9,1... | collective-permute-start | bytes 1544 | tf_op jit(solution)/shard_map/ppermute | solution.py:18
  15.8 1.6 %collective-permute-start = (s32[128]{0:T(128)S(1)}, s32[128]{0:T(128)S(1)}, u32[]{:S(2)}, u32[]{:S(2)}) collective-permute-start(s32[128]{0:T(128)S(1)} %bitcast.20), channel_id=1, source_target_pairs={{0,1},{1,0},{2,3},{3,2},{4,5},{5,4},{6,7},{7,6},{8,9},{9,8},{10,11... | collective-permute-start | bytes 1544 | tf_op jit(solution)/shard_map/ppermute | solution.py:18
  17.4 0.0 copy-done.1
  17.4 0.0 copy-done.2
  17.4 0.2 subtract_bitcast_fusion
  17.6 0.6 gather_fusion
  18.3 2.2 %gather_fusion.1 = f32[128,128]{1,0:T(8,128)S(1)} fusion(f32[4096,128]{1,0:T(8,128)} %bitcast.14, s32[1024]{0:T(1024)S(1)} %pad_clamp_fusion), kind=kCustom, calls=%fused_computation.1 | custom fusion | bytes 131584 | tf_op jit(solution)/shard_map/gather | solution.py:26
  20.5 0.4 collective-permute-start.3
  20.9 0.9 collective-permute-start.1
  21.9 4.1 %scatter_custom_fusion.2 = f32[4096,128]{1,0:T(8,128)} fusion(f32[4096,128]{1,0:T(8,128)} %bitcast.15, s32[128]{0:T(128)S(1)} %fusion.8, bf16[128,128]{1,0:T(8,128)(2,1)S(1)} %subtract_convert_fusion), kind=kCustom, calls=%fused_computation.13 | custom fusion | flops 32768 | bytes 2129920 | tf_op jit(solution)/shard_map/scatter-add | solution.py:27
  25.9 0.0 collective-permute-done.2
  25.9 0.0 collective-permute-done
  25.9 0.0 collective-permute-done.1
  26.0 4.1 %scatter_custom_fusion = f32[4096,128]{1,0:T(8,128)} fusion(f32[4096,128]{1,0:T(8,128)} %bitcast.17, s32[128]{0:T(128)S(1)} %compare_select_fusion.2, bf16[128,128]{1,0:T(8,128)(2,1)S(1)} %collective-permute-done.1), kind=kCustom, calls=%fused_computation.17 | custom fusion | flops 32768 | bytes 2129920 | tf_op jit(solution)/shard_map/scatter-add | solution.py:33
  30.0 0.0 collective-permute-done.3
  30.0 4.1 %scatter_custom_fusion.1 = f32[4096,128]{1,0:T(8,128)} fusion(f32[4096,128]{1,0:T(8,128)} %scatter_custom_fusion, s32[128]{0:T(128)S(1)} %compare_select_fusion, bf16[128,128]{1,0:T(8,128)(2,1)S(1)} %collective-permute-done.3), kind=kCustom, calls=%fused_computation.15 | custom fusion | flops 32768 | bytes 2129920 | tf_op jit(solution)/shard_map/scatter-add | solution.py:33
  34.1 3.6 %fusion.9 = bf16[4096,128]{1,0:T(8,128)(2,1)} fusion(f32[4096,128]{1,0:T(8,128)S(1)} %subtract_bitcast_fusion, f32[4096,128]{1,0:T(8,128)} %scatter_custom_fusion.1, f32[4096,128]{1,0:T(8,128)} %scatter_custom_fusion.2), kind=kLoop, calls=%fused_computation.25 | loop fusion | flops 2621440 | bytes 7340032 | tf_op jit(solution)/shard_map/convert_element_type | solution.py:39
  37.6 0.0 reduce-scatter.2.cloned.1.call-update
  37.7 0.0 all-gather.2.cloned.1.call-start
  37.7 28.2 %reduce-scatter.2.cloned.1.call-done = bf16[1024,128]{1,0:T(8,128)(2,1)} async-done(((bf16[4096,128]{1,0:T(8,128)(2,1)}), bf16[1024,128]{1,0:T(8,128)(2,1)}) %reduce-scatter.2.cloned.1.call-update) | async-done | bytes 262160 | tf_op jit(solution)/shard_map/reduce_scatter | solution.py:38
  65.9 1.0 fusion
  66.9 1.5 %collective-permute-start.6 = (bf16[1024,128]{1,0:T(8,128)(2,1)S(1)}, bf16[1024,128]{1,0:T(8,128)(2,1)S(1)}, u32[]{:S(2)}, u32[]{:S(2)}) collective-permute-start(bf16[1024,128]{1,0:T(8,128)(2,1)S(1)} %fusion), channel_id=1, source_target_pairs={{0,16},{16,0},{4,20},{20,4},{8,24},{24,8},{12,28},{28,12},{1,17},{... | collective-permute-start | bytes 786440 | tf_op jit(solution)/shard_map/ppermute | solution.py:18
  68.4 1.5 %collective-permute-start.5 = (bf16[1024,128]{1,0:T(8,128)(2,1)S(1)}, bf16[1024,128]{1,0:T(8,128)(2,1)S(1)}, u32[]{:S(2)}, u32[]{:S(2)}) collective-permute-start(bf16[1024,128]{1,0:T(8,128)(2,1)S(1)} %fusion), channel_id=1, source_target_pairs={{0,8},{8,0},{4,12},{12,4},{16,24},{24,16},{20,28},{28,20},{1,9},{9... | collective-permute-start | bytes 786440 | tf_op jit(solution)/shard_map/ppermute | solution.py:18
  69.9 0.0 collective-permute-start.4
  69.9 4.7 %collective-permute-done.6 = bf16[1024,128]{1,0:T(8,128)(2,1)S(1)} collective-permute-done((bf16[1024,128]{1,0:T(8,128)(2,1)S(1)}, bf16[1024,128]{1,0:T(8,128)(2,1)S(1)}, u32[]{:S(2)}, u32[]{:S(2)}) %collective-permute-start.6) | collective-permute-done | bytes 262176 | tf_op jit(solution)/shard_map/ppermute | solution.py:18
  74.6 1.2 collective-permute-done.5
  75.8 0.0 collective-permute-done.4
  75.8 2.5 %multiply_reduce_fusion = (f32[]{:T(128)}, bf16[1024,128]{1,0:T(8,128)(2,1)}) fusion(bf16[1024,128]{1,0:T(8,128)(2,1)S(1)} %collective-permute-done.6, bf16[1024,128]{1,0:T(8,128)(2,1)S(1)} %collective-permute-done.5, bf16[1024,128]{1,0:T(8,128)(2,1)S(1)} %collective-permute-done.4, bf16[1024,128]{1,0:T(8,128)(2,1)} %reduce-scatter.2.cloned.1.call-done), kind=kLoop, calls=%fused_computation.8 | loop fusion | flops 1703935 | bytes 1310724 | tf_op jit(solution)/shard_map/reduce_sum | solution.py:49
  78.3 0.0 all-gather.2.cloned.1.call-update
  78.3 39.7 %psum.7 = f32[]{:T(128)} all-reduce(f32[]{:T(128)} %get-tuple-element.4), channel_id=1, replica_groups=mesh['grp'=8,'cube'=4] {'grp','cube'}, use_global_device_ids=true, to_apply=%region_5.0 | all-reduce | flops 1 | bytes 8 | tf_op jit(solution)/shard_map/psum | solution.py:49
  118.7 0.0 all-gather.2.cloned.1.call-done
  118.7 4.3 %add_bitcast_fusion = f32[1,1,4096,128]{3,2,1,0:T(8,128)} fusion(bf16[4096,128]{1,0:T(8,128)(2,1)} %all-gather.2.cloned.1.call-done, f32[4096,128]{1,0:T(8,128)S(1)} %subtract_bitcast_fusion, f32[4096,128]{1,0:T(8,128)} %scatter_custom_fusion.1, f32[4096,128]{1,0:T(8,128)} %scatter_custom_fusion.2), kind=kLoop, calls=%fused_computation.5 | loop fusion | flops 3670016 | bytes 9437184 | tf_op jit(solution)/shard_map/broadcast_in_dim | solution.py:56
  (5 shorter events, 0.0 us)
Async XLA Ops:
  7.2 3.2 %copy-start = (f32[1,1,4096,128]{3,2,1,0:T(8,128)S(1)}, f32[1,1,4096,128]{3,2,1,0:T(8,128)}, u32[]{:S(2)}) copy-start(f32[1,1,4096,128]{3,2,1,0:T(8,128)} %param.7) | copy-start | bytes 6291460
  7.2 58.7 %reduce-scatter.2.cloned.1.call-start = ((), (), s32[]{:S(2)}) async-start(), calls=%async_computation.1 | async-start | bytes 1310720 | tf_op jit(solution)/shard_map/reduce_scatter | solution.py:38
  10.4 1.3 %copy-start.3 = (s32[1,1,128]{2,1,0:T(1,128)S(1)}, s32[1,1,128]{2,1,0:T(1,128)}, u32[]{:S(2)}) copy-start(s32[1,1,128]{2,1,0:T(1,128)} %param.9) | copy-start | bytes 1540
  10.4 7.0 %copy-start.1 = (f32[1,1,4096,128]{3,2,1,0:T(8,128)S(1)}, f32[1,1,4096,128]{3,2,1,0:T(8,128)}, u32[]{:S(2)}) copy-start(f32[1,1,4096,128]{3,2,1,0:T(8,128)} %param.5) | copy-start | bytes 6291460
  10.4 7.0 %copy-start.2 = (bf16[1,1,4096,128]{3,2,1,0:T(8,128)(2,1)S(1)}, bf16[1,1,4096,128]{3,2,1,0:T(8,128)(2,1)}, u32[]{:S(2)}) copy-start(bf16[1,1,4096,128]{3,2,1,0:T(8,128)(2,1)} %param.8) | copy-start | bytes 3145732
  11.7 14.2 %collective-permute-start.2 = (s32[128]{0:T(128)S(1)}, s32[128]{0:T(128)S(1)}, u32[]{:S(2)}, u32[]{:S(2)}) collective-permute-start(s32[128]{0:T(128)S(1)} %bitcast.19), channel_id=1, source_target_pairs={{0,2},{2,0},{1,3},{3,1},{4,6},{6,4},{5,7},{7,5},{8,10},{10,8},{9,1... | collective-permute-start | bytes 1544 | tf_op jit(solution)/shard_map/ppermute | solution.py:18
  15.8 10.1 %collective-permute-start = (s32[128]{0:T(128)S(1)}, s32[128]{0:T(128)S(1)}, u32[]{:S(2)}, u32[]{:S(2)}) collective-permute-start(s32[128]{0:T(128)S(1)} %bitcast.20), channel_id=1, source_target_pairs={{0,1},{1,0},{2,3},{3,2},{4,5},{5,4},{6,7},{7,6},{8,9},{9,8},{10,11... | collective-permute-start | bytes 1544 | tf_op jit(solution)/shard_map/ppermute | solution.py:18
  20.5 9.5 %collective-permute-start.3 = (bf16[128,128]{1,0:T(8,128)(2,1)S(1)}, bf16[128,128]{1,0:T(8,128)(2,1)S(1)}, u32[]{:S(2)}, u32[]{:S(2)}) collective-permute-start(bf16[128,128]{1,0:T(8,128)(2,1)S(1)} %subtract_convert_fusion), channel_id=1, source_target_pairs={{0,2},{2,0},{1,3},{3,1},{4,6},{6,4},{5,7},{7,5},{8,10},{10,8},{9,1... | collective-permute-start | bytes 98312 | tf_op jit(solution)/shard_map/ppermute | solution.py:18
  20.9 5.0 %collective-permute-start.1 = (bf16[128,128]{1,0:T(8,128)(2,1)S(1)}, bf16[128,128]{1,0:T(8,128)(2,1)S(1)}, u32[]{:S(2)}, u32[]{:S(2)}) collective-permute-start(bf16[128,128]{1,0:T(8,128)(2,1)S(1)} %subtract_convert_fusion), channel_id=1, source_target_pairs={{0,1},{1,0},{2,3},{3,2},{4,5},{5,4},{6,7},{7,6},{8,9},{9,8},{10,11... | collective-permute-start | bytes 98312 | tf_op jit(solution)/shard_map/ppermute | solution.py:18
  37.7 81.0 %all-gather.2.cloned.1.call-start = ((), (), s32[]{:S(2)}) async-start(), calls=%async_computation.2 | async-start | bytes 1310720 | tf_op jit(solution)/shard_map/all_gather | solution.py:50
  66.9 7.7 %collective-permute-start.6 = (bf16[1024,128]{1,0:T(8,128)(2,1)S(1)}, bf16[1024,128]{1,0:T(8,128)(2,1)S(1)}, u32[]{:S(2)}, u32[]{:S(2)}) collective-permute-start(bf16[1024,128]{1,0:T(8,128)(2,1)S(1)} %fusion), channel_id=1, source_target_pairs={{0,16},{16,0},{4,20},{20,4},{8,24},{24,8},{12,28},{28,12},{1,17},{... | collective-permute-start | bytes 786440 | tf_op jit(solution)/shard_map/ppermute | solution.py:18
  68.4 7.4 %collective-permute-start.5 = (bf16[1024,128]{1,0:T(8,128)(2,1)S(1)}, bf16[1024,128]{1,0:T(8,128)(2,1)S(1)}, u32[]{:S(2)}, u32[]{:S(2)}) collective-permute-start(bf16[1024,128]{1,0:T(8,128)(2,1)S(1)} %fusion), channel_id=1, source_target_pairs={{0,8},{8,0},{4,12},{12,4},{16,24},{24,16},{20,28},{28,20},{1,9},{9... | collective-permute-start | bytes 786440 | tf_op jit(solution)/shard_map/ppermute | solution.py:18
  69.9 5.9 %collective-permute-start.4 = (bf16[1024,128]{1,0:T(8,128)(2,1)S(1)}, bf16[1024,128]{1,0:T(8,128)(2,1)S(1)}, u32[]{:S(2)}, u32[]{:S(2)}) collective-permute-start(bf16[1024,128]{1,0:T(8,128)(2,1)S(1)} %fusion), channel_id=1, source_target_pairs={{0,4},{4,0},{8,12},{12,8},{16,20},{20,16},{24,28},{28,24},{1,5},{5... | collective-permute-start | bytes 786440 | tf_op jit(solution)/shard_map/ppermute | solution.py:18
Sparse Core Ops, SparseCore 0:
  37.8 28.0 reduce-scatter.1
  78.4 26.6 all-gather.1
where the time goes:
time: 131 us
  blocking collectives  39.7 us (30%)
  waiting for transfers between devices  34.1 us (26%)
  other arithmetic  23.8 us (18%)
  between operations  15.9 us (12%)
  starting transfers between devices  10 us (8%)
  local copies, waits for them, and re-layouts  7.4 us (6%)
    psum x1, blocking collectives, local(): spread_sum = lax.psum(jnp.sum(shortfall * shortfall), ('grp', 'cube'))  39.7 us
    reduce_scatter x1, waiting for transfers between devices, local(): lax.psum_scatter(mixed_in.astype(jnp.bfloat16), 'cube', scatter_dimension...  28.2 us
    ppermute x7, starting transfers between devices, partner(): return lax.ppermute(block, axis, route)  9.96 us
    scatter-add x2, other arithmetic, local(): summed = summed.at[their_rows].add(their_values.astype(jnp.float32))  8.12 us
    ppermute x7, waiting for transfers between devices, partner(): return lax.ppermute(block, axis, route)  5.92 us
    unnamed x10, local copies, waits for them, and re-layouts  4.52 us
    broadcast_in_dim x1, other arithmetic, local(): new_params[None, None]  4.34 us
    scatter-add x1, other arithmetic, local(): new_estimate = current.at[chosen].add(picked.astype(jnp.float32))  4.05 us
  transfers between devices with their start and end apart: 9, of which 3 were waited for; matrix products, arithmetic and copies ran while one was open for 9% of the time, Pallas kernels for 0%

commit v1 on v0

v1 whole, which is shorter than its diff:
```python
import functools

import jax
import jax.numpy as jnp
from jax import lax
from jax.experimental import pallas as pl
from jax.experimental.pallas import tpu as pltpu
from jax.sharding import PartitionSpec as P

LEARN_RATE = 0.1
INNER_RATE = 0.6
OUTER_RATE = 0.5
CHUNK = 256
ENDS = 6
HOP = 2
SWAP = 2
BACK = 2
PIECES = 4

MESH = pl.DeviceIdType.MESH
F32, BF16 = jnp.float32, jnp.bfloat16


def kernel(
    n_cube, n_grp,
    params, estimate, neighbour_sum, gradient, ids,
    p_v, e_v, n_v, consensus,
    g_v, picked, theirs, their_ids,
    from_left, from_right, outgoing, mean_out, mean_in, fix, shortfall_v,
    spread, spread_grp, spread_cube,
    load_sem, pick_send, pick_recv, id_send, id_recv,
    up_send, left_recv, right_recv, mean_send, mean_recv,
    fix_send, fix_recv,
    sg_send, sg_recv, sc_send, sc_recv,
):
    me, grp = lax.axis_index("cube"), lax.axis_index("grp")
    rows, width = p_v.shape
    kept = picked.shape[0]
    chunks = rows // CHUNK
    cube_bits, grp_bits = n_cube.bit_length() - 1, n_grp.bit_length() - 1
    piece = rows // PIECES

    def load(which, at):
        src, dst = ((params, p_v), (gradient, g_v), (estimate, e_v), (neighbour_sum, n_v))[which]
        window = pl.ds(at * piece, piece)
        return pltpu.make_async_copy(src.at[window], dst.at[window], load_sem.at[which, at])

    for at in range(PIECES):
        for which in range(3):
            load(which, at).start()
    for at in range(PIECES):
        load(3, at).start()

    barrier = pltpu.get_barrier_semaphore()
    for d in range(1, n_cube):
        pl.semaphore_signal(barrier, inc=1, device_id={"cube": (me + d) % n_cube}, device_id_type=MESH)
    for d in range(1, n_grp):
        pl.semaphore_signal(barrier, inc=1, device_id={"grp": (grp + d) % n_grp}, device_id_type=MESH)
    pl.semaphore_wait(barrier, n_cube + n_grp - 2)

    def flip(index, level):
        bit = 1 << level
        return index + bit - 2 * bit * ((index // bit) % 2)

    def copy(src, dst, send, recv, **device):
        return pltpu.make_async_remote_copy(
            src_ref=src, dst_ref=dst, send_sem=send, recv_sem=recv, device_id=device, device_id_type=MESH
        )

    def id_copy(level):
        return copy(ids, their_ids.at[level], id_send.at[level], id_recv.at[level], cube=flip(me, level))

    def pick_copy(level):
        return copy(
            picked, theirs.at[pl.ds(level * kept, kept)], pick_send.at[level], pick_recv.at[level],
            cube=flip(me, level),
        )

    for level in range(cube_bits):
        id_copy(level).start()

    square = (kept, kept)
    own_ids = ids[...]
    diagonal = lax.broadcasted_iota(jnp.int32, square, 0) == lax.broadcasted_iota(jnp.int32, square, 1)
    id_column = jnp.sum(jnp.where(diagonal, jnp.broadcast_to(own_ids, square), 0), axis=1, keepdims=True)

    def pick(j, total):
        window = pl.ds(pl.multiple_of(j * CHUNK, CHUNK), CHUNK)
        stepped = p_v[window, :] - LEARN_RATE * g_v[window, :].astype(F32)
        p_v[window, :] = stepped
        change = (stepped - e_v[window, :]).astype(BF16)
        row = lax.broadcasted_iota(jnp.int32, (kept, CHUNK), 1) + j * CHUNK
        hot = (row == id_column).astype(F32).astype(BF16)
        return total + jnp.dot(hot, change, preferred_element_type=F32)

    total = jnp.zeros((kept, width), F32)
    for at in range(PIECES):
        for which in range(3):
            load(which, at).wait()
        each = piece // CHUNK
        total = lax.fori_loop(at * each, (at + 1) * each, pick, total)
    picked[...] = total.astype(BF16)
    for level in range(cube_bits):
        pick_copy(level).start()
    for at in range(PIECES):
        load(3, at).wait()
    spread[...] = jnp.zeros_like(spread)
    for level in range(cube_bits):
        id_copy(level).wait()
    for level in range(cube_bits):
        pick_copy(level).wait()

    def window_of(j):
        return pl.ds(pl.multiple_of(j * CHUNK, CHUNK), CHUNK)

    def mix(j):
        window = window_of(j)
        row = lax.broadcasted_iota(jnp.int32, (CHUNK, kept), 0) + j * CHUNK

        def hot(names):
            return (row == names).astype(F32).astype(BF16)

        e = e_v[window, :] + jnp.dot(hot(own_ids), picked[...], preferred_element_type=F32)
        marks = jnp.concatenate([hot(their_ids[level]) for level in range(cube_bits)], axis=1)
        s = n_v[window, :] + jnp.dot(marks, theirs[...], preferred_element_type=F32)
        e_v[window, :] = e
        n_v[window, :] = s
        p_v[window, :] = p_v[window, :] + (INNER_RATE / (cube_bits + 1)) * (s - cube_bits * e)

    low, high = n_cube // 2 - 1, n_cube // 2
    owners = sorted({0, n_cube - 1, low, high})

    def owner(j):
        return jnp.where(j < ENDS, (j % 2) * (n_cube - 1), low + j % 2)

    def valid(j):
        return jnp.logical_and(j >= 0, j < chunks)

    def right_copy(j):
        return copy(outgoing.at[j], from_left.at[j], up_send.at[j], left_recv.at[j], cube=me + 1)

    def left_copy(j):
        return copy(outgoing.at[j], from_right.at[j], up_send.at[j], right_recv.at[j], cube=me - 1)

    def wait_left(j):
        copy(from_left.at[j], from_left.at[j], up_send.at[j], left_recv.at[j], cube=me).wait_recv()

    def wait_right(j):
        copy(from_right.at[j], from_right.at[j], up_send.at[j], right_recv.at[j], cube=me).wait_recv()

    def mean_copy(level, j):
        return copy(
            mean_out.at[j], mean_in.at[level, j], mean_send.at[level, j], mean_recv.at[level, j],
            grp=flip(grp, level),
        )

    def fix_copy(side, j):
        return copy(fix.at[j], fix.at[j], fix_send.at[side, j], fix_recv.at[j], cube=me + (1 if side else -1))

    def finish(j, amount):
        p_v[window_of(j), :] = p_v[window_of(j), :] + OUTER_RATE * amount

    def spread_copy_grp(d):
        return copy(
            spread, spread_grp.at[grp], sg_send.at[d], sg_recv.at[grp], grp=(grp + d) % n_grp
        )

    def spread_copy_cube(d):
        return copy(
            spread_grp.at[n_grp], spread_cube.at[me], sc_send.at[d], sc_recv.at[me], cube=(me + d) % n_cube
        )

    def climb(step):
        j = step - me * HOP

        @pl.when(valid(j))
        def _():
            @pl.when(me < owner(j))
            def _():
                @pl.when(me > 0)
                def _():
                    wait_left(j)
                    outgoing[j] = (p_v[window_of(j), :] + from_left[j].astype(F32)).astype(BF16)

                @pl.when(me == 0)
                def _():
                    outgoing[j] = p_v[window_of(j), :].astype(BF16)

                right_copy(j).start()

        i = step - (n_cube - 1 - me) * HOP

        @pl.when(valid(i))
        def _():
            @pl.when(me > owner(i))
            def _():
                @pl.when(me < n_cube - 1)
                def _():
                    wait_right(i)
                    outgoing[i] = (p_v[window_of(i), :] + from_right[i].astype(F32)).astype(BF16)

                @pl.when(me == n_cube - 1)
                def _():
                    outgoing[i] = p_v[window_of(i), :].astype(BF16)

                left_copy(i).start()

    def reach(at):
        return max(at, n_cube - 1 - at) * HOP

    my_reach = jnp.where(2 * me < n_cube, n_cube - 1 - me, me) * HOP

    def own(step):
        j = step - my_reach

        @pl.when(valid(j))
        def _():
            @pl.when(me == owner(j))
            def _():
                shortfall_v[j] = p_v[window_of(j), :]

                @pl.when(me > 0)
                def _():
                    wait_left(j)
                    shortfall_v[j] = shortfall_v[j] + from_left[j].astype(F32)

                @pl.when(me < n_cube - 1)
                def _():
                    wait_right(j)
                    shortfall_v[j] = shortfall_v[j] + from_right[j].astype(F32)

                mean = shortfall_v[j] * (1.0 / n_cube)
                shortfall_v[j] = mean
                mean_out[j] = mean.astype(BF16)
                for level in range(grp_bits):
                    mean_copy(level, j).start()

    def settle(step):
        j = step - my_reach - SWAP

        @pl.when(valid(j))
        def _():
            @pl.when(me == owner(j))
            def _():
                mean = shortfall_v[j]
                combined = mean
                for level in range(grp_bits):
                    mean_copy(level, j).wait_recv()
                    combined = combined + mean_in[level, j].astype(F32)
                shortfall = combined * (1.0 / (grp_bits + 1)) - mean
                fix[j] = shortfall.astype(BF16)

                @pl.when(me > 0)
                def _():
                    fix_copy(0, j).start()

                @pl.when(me < n_cube - 1)
                def _():
                    fix_copy(1, j).start()

                spread[...] += jnp.sum((shortfall * shortfall).reshape(CHUNK // 8, 8, width), axis=0)
                finish(j, shortfall)

    def descend(step, at):
        away = jnp.where(me < at, at - me, me - at)
        j = step - reach(at) - SWAP - away * BACK

        @pl.when(jnp.logical_and(valid(j), me != at))
        def _():
            @pl.when(owner(j) == at)
            def _():
                copy(fix.at[j], fix.at[j], fix_send.at[0, j], fix_recv.at[j], cube=me).wait_recv()
                if at > 1:
                    @pl.when(jnp.logical_and(me < at, me > 0))
                    def _():
                        fix_copy(0, j).start()
                if at < n_cube - 2:
                    @pl.when(jnp.logical_and(me > at, me < n_cube - 1))
                    def _():
                        fix_copy(1, j).start()
                finish(j, fix[j].astype(F32))

    last_settle = max(chunks - 1 + reach(high), min(ENDS, chunks) - 1 + reach(0)) + SWAP
    last_step = max(
        chunks - 1 + reach(high) + high * BACK, min(ENDS, chunks) - 1 + reach(0) + (n_cube - 1) * BACK
    ) + SWAP

    def run(step, carry):
        @pl.when(step < chunks)
        def _():
            mix(step)

        climb(step)
        own(step)
        settle(step)
        @pl.when(step == last_settle)
        def _():
            spread_grp[grp] = spread[...]
            for d in range(1, n_grp):
                spread_copy_grp(d).start()

        for at in owners:
            descend(step, at)
        return carry

    lax.fori_loop(0, last_step + 1, run, 0)

    for d in range(1, n_grp):
        src = (grp + d) % n_grp
        copy(spread_grp.at[src], spread_grp.at[src], sg_send.at[d], sg_recv.at[src], grp=grp).wait_recv()
    here = jnp.sum(spread_grp[pl.ds(0, n_grp)], axis=0)
    spread_grp[n_grp] = here
    spread_cube[me] = here
    for d in range(1, n_cube):
        spread_copy_cube(d).start()

    def drain(j, carry):
        o = owner(j)

        @pl.when(me != o)
        def _():
            copy(outgoing.at[j], outgoing.at[j], up_send.at[j], left_recv.at[j], cube=me).wait_send()

        @pl.when(me == o)
        def _():
            for level in range(grp_bits):
                mean_copy(level, j).wait_send()

        @pl.when(jnp.logical_and(me <= o, me > 0))
        def _():
            fix_copy(0, j).wait_send()

        @pl.when(jnp.logical_and(me >= o, me < n_cube - 1))
        def _():
            fix_copy(1, j).wait_send()

        return carry

    lax.fori_loop(0, chunks, drain, 0)
    for d in range(1, n_grp):
        spread_copy_grp(d).wait_send()
    for d in range(1, n_cube):
        src = (me + d) % n_cube
        copy(spread_cube.at[src], spread_cube.at[src], sc_send.at[d], sc_recv.at[src], cube=me).wait_recv()
        spread_copy_cube(d).wait_send()
    whole = jnp.sum(spread_cube[...], axis=0)
    whole = jnp.sum(jnp.sum(whole, axis=0, keepdims=True), axis=1, keepdims=True)
    consensus[...] = jnp.broadcast_to(jnp.sqrt(whole / (n_grp * rows * width)), consensus.shape)


def local(params, estimate, neighbour_sum, gradient, block_ids):
    n_cube, n_grp = lax.axis_size("cube"), lax.axis_size("grp")
    rows, width = params.shape[2:]
    kept = block_ids.shape[2]
    cube_bits, grp_bits = n_cube.bit_length() - 1, n_grp.bit_length() - 1
    chunks = rows // CHUNK
    slab = jax.ShapeDtypeStruct((rows, width), F32)
    dma = pltpu.SemaphoreType.DMA
    pieces = (chunks, CHUNK, width)
    hbm = pl.BlockSpec(memory_space=pltpu.HBM)
    vmem = pl.BlockSpec(memory_space=pltpu.VMEM)
    out = pl.pallas_call(
        functools.partial(kernel, n_cube, n_grp),
        out_shape=(slab, slab, slab, jax.ShapeDtypeStruct((1, width), F32)),
        in_specs=[hbm] * 4 + [vmem],
        out_specs=(vmem,) * 4,
        scratch_shapes=[
            pltpu.VMEM((rows, width), BF16),
            pltpu.VMEM((kept, width), BF16),
            pltpu.VMEM((cube_bits * kept, width), BF16),
            pltpu.VMEM((cube_bits, 1, kept), jnp.int32),
            pltpu.VMEM(pieces, BF16),
            pltpu.VMEM(pieces, BF16),
            pltpu.VMEM(pieces, BF16),
            pltpu.VMEM(pieces, BF16),
            pltpu.VMEM((grp_bits,) + pieces, BF16),
            pltpu.VMEM(pieces, BF16),
            pltpu.VMEM(pieces, F32),
            pltpu.VMEM((8, width), F32),
            pltpu.VMEM((n_grp + 1, 8, width), F32),
            pltpu.VMEM((n_cube, 8, width), F32),
            dma((4, PIECES)),
            dma((cube_bits,)),
            dma((cube_bits,)),
            dma((cube_bits,)),
            dma((cube_bits,)),
            dma((chunks,)),
            dma((chunks,)),
            dma((chunks,)),
            dma((grp_bits, chunks)),
            dma((grp_bits, chunks)),
            dma((2, chunks)),
            dma((chunks,)),
            dma((n_grp,)),
            dma((n_grp,)),
            dma((n_cube,)),
            dma((n_cube,)),
        ],
        compiler_params=pltpu.CompilerParams(
            collective_id=0, has_side_effects=True, vmem_limit_bytes=40 * 1024 * 1024
        ),
    )(
        *(
            pltpu.with_memory_space_constraint(slab[0, 0], pltpu.HBM)
            for slab in (params, estimate, neighbour_sum, gradient)
        ),
        block_ids[0],
    )
    return (out[0][None, None], out[1][None, None], out[2][None, None], out[3][0, :1])


def solution(mesh):
    in_specs = (
        P("grp", "cube", None, None),
        P("grp", "cube", None, None),
        P("grp", "cube", None, None),
        P("grp", "cube", None, None),
        P("grp", "cube", None),
    )
    out_specs = (
        P("grp", "cube", None, None),
        P("grp", "cube", None, None),
        P("grp", "cube", None, None),
        P(),
    )
    return jax.shard_map(local, mesh=mesh, in_specs=in_specs, out_specs=out_specs, check_vma=False)
```

time: 131 us -> 67.8 us (0.52)
  Pallas kernels: 0 us -> 61.2 us
  blocking collectives: 39.7 us -> 0 us
  waiting for transfers between devices: 34.1 us -> 0 us
  other arithmetic: 23.8 us -> 0 us
  between operations: 15.9 us -> 1.81 us
  starting transfers between devices: 10 us -> 0 us
  local copies, waits for them, and re-layouts: 7.4 us -> 4.61 us
    pallas_call x0 -> x1, Pallas kernels: none -> 61.2 us  [local(): pl.pallas_call(functools.partial(kernel, n_cube, n_grp), out_shape=(slab,...]
    psum x1 -> x0, blocking collectives: 39.7 us -> none  [local(): spread_sum = lax.psum(jnp.sum(shortfall * shortfall), ('grp', 'cube'))]
    reduce_scatter x1 -> x0, waiting for transfers between devices: 28.2 us -> none  [local(): lax.psum_scatter(mixed_in.astype(jnp.bfloat16), 'cube', scatter_dimension...]
    scatter-add x3 -> x0, other arithmetic: 12.2 us -> none  [the longest x2 8.12 us: local(): summed = summed.at[their_rows].add(their_values.astype(jnp.float32))]
    ppermute x7 -> x0, starting transfers between devices: 9.96 us -> none  [partner(): return lax.ppermute(block, axis, route)]
    ppermute x7 -> x0, waiting for transfers between devices: 5.92 us -> none  [partner(): return lax.ppermute(block, axis, route)]
    convert_element_type x3 -> x0, other arithmetic: 4.58 us -> none  [the longest x1 3.57 us: local(): mixed_in.astype(jnp.bfloat16)]
    broadcast_in_dim x1 -> x0, other arithmetic: 4.34 us -> none  [local(): new_params[None, None]]
  transfers between devices with their start and end apart: 9 -> 0, of which waited for: 3 -> 0; matrix products, arithmetic and copies ran while one was open for 9% -> 0% of each run, Pallas kernels for 0% -> 0%
where the time goes in v1:
time: 67.8 us; the launch traced here: 67.6 us
  Pallas kernels  61.2 us (90%)
  local copies, waits for them, and re-layouts  4.61 us (7%)
  between operations  1.81 us (3%)
    pallas_call x1, Pallas kernels, local(): pl.pallas_call(functools.partial(kernel, n_cube, n_grp), out_shape=(slab,...  61.2 us
    unnamed x5, local copies, waits for them, and re-layouts  4.61 us

profile of v1, /device:TPU:0, one launch (start us, length us, event | category | flops | bytes accessed | tf_op | source)
XLA Modules:
  0.0 67.6 jit_solution(11852975514154511388)
XLA Ops:
  0.6 0.0 copy-start
  0.6 0.6 copy-done
  1.3 61.2 %shard_map.84 = (f32[4096,128]{1,0:T(8,128)S(1)}, f32[4096,128]{1,0:T(8,128)S(1)}, f32[4096,128]{1,0:T(8,128)S(1)}, f32[1,128]{1,0:T(1,128)S(1)}) custom-call(f32[4096,128]{1,0:T(8,128)} %bitcast.15, f32[4096,128]{1,0:T(8,128)} %bitcast.16, f32[4096,128]{1,0:T(8,128)} %bitcast.17, bf16[4096,128]{1,0:T(8,128)(2,1)} %bitcast.18, s32[1,128]{1,0:T(1,128)S(1)} %bitcast.13), custom_call_target="tpu_custom_call" | custom-call | tf_op jit(solution)/shard_map/pallas_call | solution.py:362
  62.5 1.3 %copy.13 = f32[1,1,4096,128]{3,2,1,0:T(8,128)} copy(f32[1,1,4096,128]{3,2,1,0:T(8,128)S(1)} %bitcast.12) | data formatting | bytes 4194304
  63.8 1.3 %copy.14 = f32[1,1,4096,128]{3,2,1,0:T(8,128)} copy(f32[1,1,4096,128]{3,2,1,0:T(8,128)S(1)} %bitcast.11) | data formatting | bytes 4194304
  65.1 1.3 %copy.15 = f32[1,1,4096,128]{3,2,1,0:T(8,128)} copy(f32[1,1,4096,128]{3,2,1,0:T(8,128)S(1)} %bitcast.10) | data formatting | bytes 4194304
Async XLA Ops:
  0.6 0.7 copy-start

commit v2 on v1

v2 whole, which is shorter than its diff:
```python
import functools
import heapq

import jax
import jax.numpy as jnp
from jax import lax
from jax.experimental import pallas as pl
from jax.experimental.pallas import tpu as pltpu
from jax.sharding import PartitionSpec as P

LEARN_RATE = 0.1
INNER_RATE = 0.6
OUTER_RATE = 0.5
CHUNK = 128
ENDS = 16
WIRE = 0.7
DELAY = 2.0
LATE = 3.0
BLOCK = 128
PIECES = 4

MESH = pl.DeviceIdType.MESH
F32, BF16 = jnp.float32, jnp.bfloat16


def owner_of(j, n_cube):
    if j < ENDS and j % 4 >= 2:
        return (j % 2) * (n_cube - 1)
    return n_cube // 2 - 1 + j % 2


def plan(n_cube, chunks):
    work, order, busy, link = [], [[] for _ in range(n_cube)], [0.0] * n_cube, {}
    met, last = {}, [0.0] * n_cube
    count = 0

    def push(at, device, kind, j):
        nonlocal count
        heapq.heappush(work, (at, count, device, kind, j))
        count += 1

    def send(at, device, to, scale=1.0):
        key = (device, to)
        link[key] = max(at, link.get(key, 0.0)) + WIRE * scale
        return link[key] + DELAY

    for device in range(n_cube):
        for j in range(chunks):
            push(0.25 * j, device, "mix", j)
    started = [0] * n_cube

    def meet(at, device, j):
        o = owner_of(j, n_cube)
        key = (device, j)
        need = 1 + (device > 0) + (device < n_cube - 1) if device == o else 1 + (0 < device < n_cube - 1)
        seen = met.setdefault(key, [])
        seen.append(at)
        if len(seen) == need:
            push(max(seen), device, "own" if device == o else "climb", j)

    while work:
        at, _, device, kind, j = heapq.heappop(work)
        if at < busy[device]:
            push(busy[device], device, kind, j)
            continue
        order[device].append((kind, j))
        busy[device] = at + (0.25 if kind == "mix" else 0.15)
        now = busy[device]
        o = owner_of(j, n_cube)
        if kind == "mix":
            first = device in (0, n_cube - 1) and device != o
            meet(max(now, 0.9 * WIRE * started[device]) if first else now, device, j)
            started[device] += first
        elif kind == "climb":
            to = device + 1 if device < o else device - 1
            meet(send(now, device, to), to, j)
        elif kind == "own":
            late = LATE if device in (0, n_cube - 1) else 0.0
            push(send(now, device, "swap") + late, device, "settle", j)
        else:
            if kind == "settle":
                last[device] = now
            if device <= o and device > 0:
                push(send(now, device, device - 1), device - 1, "descend", j)
            if device >= o and device < n_cube - 1:
                push(send(now, device, device + 1), device + 1, "descend", j)
    return order


def kernel(
    n_cube, n_grp,
    params, estimate, neighbour_sum, gradient, ids,
    p_v, e_v, n_v, consensus,
    g_v, picked, theirs, their_ids,
    from_left, from_right, outgoing, mean_out, mean_in, fix, shortfall_v,
    spread, spread_grp, spread_cube,
    load_sem, pick_send, pick_recv, id_send, id_recv,
    up_send, left_recv, right_recv, mean_send, mean_recv,
    fix_send, fix_recv,
    sg_send, sg_recv, sc_send, sc_recv,
):
    me, grp = lax.axis_index("cube"), lax.axis_index("grp")
    rows, width = p_v.shape
    kept = picked.shape[0]
    chunks = rows // CHUNK
    cube_bits, grp_bits = n_cube.bit_length() - 1, n_grp.bit_length() - 1
    piece = rows // PIECES

    def load(which, at):
        src, dst = ((params, p_v), (gradient, g_v), (estimate, e_v), (neighbour_sum, n_v))[which]
        window = pl.ds(at * piece, piece)
        return pltpu.make_async_copy(src.at[window], dst.at[window], load_sem.at[which, at])

    barrier = pltpu.get_barrier_semaphore()
    for d in range(1, n_cube):
        pl.semaphore_signal(barrier, inc=1, device_id={"cube": (me + d) % n_cube}, device_id_type=MESH)
    for d in range(1, n_grp):
        pl.semaphore_signal(barrier, inc=1, device_id={"grp": (grp + d) % n_grp}, device_id_type=MESH)
    for at in range(PIECES):
        for which in range(3):
            load(which, at).start()
    for at in range(PIECES):
        load(3, at).start()

    def flip(index, level):
        bit = 1 << level
        return index + bit - 2 * bit * ((index // bit) % 2)

    def copy(src, dst, send, recv, **device):
        return pltpu.make_async_remote_copy(
            src_ref=src, dst_ref=dst, send_sem=send, recv_sem=recv, device_id=device, device_id_type=MESH
        )

    def id_copy(level):
        return copy(ids, their_ids.at[level], id_send.at[level], id_recv.at[level], cube=flip(me, level))

    def pick_copy(level):
        return copy(
            picked, theirs.at[pl.ds(level * kept, kept)], pick_send.at[level], pick_recv.at[level],
            cube=flip(me, level),
        )

    square = (kept, kept)
    own_ids = ids[...]
    diagonal = lax.broadcasted_iota(jnp.int32, square, 0) == lax.broadcasted_iota(jnp.int32, square, 1)
    id_column = jnp.sum(jnp.where(diagonal, jnp.broadcast_to(own_ids, square), 0), axis=1, keepdims=True)

    def pick(j, total):
        window = pl.ds(pl.multiple_of(j * CHUNK, CHUNK), CHUNK)
        stepped = p_v[window, :] - LEARN_RATE * g_v[window, :].astype(F32)
        p_v[window, :] = stepped
        change = (stepped - e_v[window, :]).astype(BF16)
        row = lax.broadcasted_iota(jnp.int32, (kept, CHUNK), 1) + j * CHUNK
        hot = (row == id_column).astype(F32).astype(BF16)
        return total + jnp.dot(hot, change, preferred_element_type=F32)

    total = jnp.zeros((kept, width), F32)
    for at in range(PIECES):
        for which in range(3):
            load(which, at).wait()
        each = piece // CHUNK
        total = lax.fori_loop(at * each, (at + 1) * each, pick, total)
    picked[...] = total.astype(BF16)
    pl.semaphore_wait(barrier, n_cube + n_grp - 2)
    for level in range(cube_bits):
        id_copy(level).start()
    for level in range(cube_bits):
        pick_copy(level).start()
    for at in range(PIECES):
        load(3, at).wait()
    spread[...] = jnp.zeros_like(spread)
    for level in range(cube_bits):
        id_copy(level).wait()
    for level in range(cube_bits):
        pick_copy(level).wait()

    def blocks(j, work):
        def one(at, carry):
            work(pl.ds(pl.multiple_of(j * CHUNK + at * BLOCK, BLOCK), BLOCK), pl.ds(pl.multiple_of(at * BLOCK, BLOCK), BLOCK))
            return carry

        lax.fori_loop(0, CHUNK // BLOCK, one, 0)

    def mix(j):
        def work(window, part):
            row = lax.broadcasted_iota(jnp.int32, (BLOCK, kept), 0) + window.start

            def hot(names):
                return (row == names).astype(F32).astype(BF16)

            e = e_v[window, :] + jnp.dot(hot(own_ids), picked[...], preferred_element_type=F32)
            marks = jnp.concatenate([hot(their_ids[level]) for level in range(cube_bits)], axis=1)
            s = n_v[window, :] + jnp.dot(marks, theirs[...], preferred_element_type=F32)
            e_v[window, :] = e
            n_v[window, :] = s
            p_v[window, :] = p_v[window, :] + (INNER_RATE / (cube_bits + 1)) * (s - cube_bits * e)

        blocks(j, work)

    across = [flip(grp, level) for level in range(grp_bits)]

    def climb_copy(role, j):
        if role < owner_of(j, n_cube):
            return copy(outgoing.at[j], from_left.at[j], up_send.at[j], left_recv.at[j], cube=role + 1)
        return copy(outgoing.at[j], from_right.at[j], up_send.at[j], right_recv.at[j], cube=role - 1)

    def wait_left(j):
        copy(from_left.at[j], from_left.at[j], up_send.at[j], left_recv.at[j], cube=me).wait_recv()

    def wait_right(j):
        copy(from_right.at[j], from_right.at[j], up_send.at[j], right_recv.at[j], cube=me).wait_recv()

    def mean_copy(level, j):
        return copy(
            mean_out.at[j], mean_in.at[level, j], mean_send.at[level, j], mean_recv.at[level, j],
            grp=across[level],
        )

    def fix_copy(side, j, to):
        return copy(fix.at[j], fix.at[j], fix_send.at[side, j], fix_recv.at[j], cube=to)

    def fix_targets(role, j):
        o = owner_of(j, n_cube)
        low = [(0, role - 1)] if role <= o and role > 0 else []
        return low + ([(1, role + 1)] if role >= o and role < n_cube - 1 else [])

    def climb(role, j):
        chain = None
        if role < owner_of(j, n_cube):
            if role > 0:
                wait_left(j)
                chain = from_left
        elif role < n_cube - 1:
            wait_right(j)
            chain = from_right

        def work(window, part):
            value = p_v[window, :]
            if chain is not None:
                value = value + chain[j, part, :].astype(F32)
            outgoing[j, part, :] = value.astype(BF16)

        blocks(j, work)
        climb_copy(role, j).start()

    def own(role, j):
        if role > 0:
            wait_left(j)
        if role < n_cube - 1:
            wait_right(j)

        def work(window, part):
            mean = p_v[window, :]
            if role > 0:
                mean = mean + from_left[j, part, :].astype(F32)
            if role < n_cube - 1:
                mean = mean + from_right[j, part, :].astype(F32)
            mean = mean * (1.0 / n_cube)
            shortfall_v[j, part, :] = mean
            mean_out[j, part, :] = mean.astype(BF16)

        blocks(j, work)
        for level in reversed(range(grp_bits)):
            mean_copy(level, j).start()

    def settle(role, j):
        for level in range(grp_bits):
            mean_copy(level, j).wait_recv()

        def work(window, part):
            mean = shortfall_v[j, part, :]
            combined = mean
            for level in range(grp_bits):
                combined = combined + mean_in[level, j, part, :].astype(F32)
            shortfall = combined * (1.0 / (grp_bits + 1)) - mean
            shortfall_v[j, part, :] = shortfall
            fix[j, part, :] = shortfall.astype(BF16)

        blocks(j, work)
        for side, to in fix_targets(role, j):
            fix_copy(side, j, to).start()

        def rest(window, part):
            shortfall = shortfall_v[j, part, :]
            spread[...] += jnp.sum((shortfall * shortfall).reshape(BLOCK // 8, 8, width), axis=0)
            p_v[window, :] = p_v[window, :] + OUTER_RATE * shortfall

        blocks(j, rest)

    def descend(role, j):
        copy(fix.at[j], fix.at[j], fix_send.at[0, j], fix_recv.at[j], cube=me).wait_recv()
        for side, to in fix_targets(role, j):
            fix_copy(side, j, to).start()

        def work(window, part):
            p_v[window, :] = p_v[window, :] + OUTER_RATE * fix[j, part, :].astype(F32)

        blocks(j, work)

    def spread_copy_grp(d):
        return copy(spread, spread_grp.at[grp], sg_send.at[d], sg_recv.at[grp], grp=(grp + d) % n_grp)

    def spread_copy_cube(d):
        return copy(
            spread_grp.at[n_grp], spread_cube.at[me], sc_send.at[d], sc_recv.at[me], cube=(me + d) % n_cube
        )

    def spread_first():
        spread_grp[grp] = spread[...]
        for d in range(1, n_grp):
            spread_copy_grp(d).start()

    def spread_second():
        for d in range(1, n_grp):
            src = (grp + d) % n_grp
            copy(spread_grp.at[src], spread_grp.at[src], sg_send.at[d], sg_recv.at[src], grp=grp).wait_recv()
        here = jnp.sum(spread_grp[pl.ds(0, n_grp)], axis=0)
        spread_grp[n_grp] = here
        spread_cube[me] = here
        for d in range(1, n_cube):
            spread_copy_cube(d).start()

    order = plan(n_cube, chunks)

    def run(role):
        steps = order[role]
        settles = [at for at, (kind, _) in enumerate(steps) if kind == "settle"]
        first = settles[-1] if settles else 0
        second = min(first + 3, len(steps) - 1)
        for at, (kind, j) in enumerate(steps):
            if kind == "mix":
                mix(j)
            else:
                {"climb": climb, "own": own, "settle": settle, "descend": descend}[kind](role, j)
            if at == first:
                spread_first()
            if at == second:
                spread_second()
        for j in range(chunks):
            if role == owner_of(j, n_cube):
                for level in range(grp_bits):
                    mean_copy(level, j).wait_send()
            else:
                climb_copy(role, j).wait_send()
            for side, to in fix_targets(role, j):
                fix_copy(side, j, to).wait_send()

    for role in range(n_cube):
        pl.when(me == role)(functools.partial(run, role))

    for d in range(1, n_grp):
        spread_copy_grp(d).wait_send()
    for d in range(1, n_cube):
        src = (me + d) % n_cube
        copy(spread_cube.at[src], spread_cube.at[src], sc_send.at[d], sc_recv.at[src], cube=me).wait_recv()
        spread_copy_cube(d).wait_send()
    whole = jnp.sum(spread_cube[...], axis=0)
    whole = jnp.sum(jnp.sum(whole, axis=0, keepdims=True), axis=1, keepdims=True)
    consensus[...] = jnp.broadcast_to(jnp.sqrt(whole / (n_grp * rows * width)), consensus.shape)


def local(params, estimate, neighbour_sum, gradient, block_ids):
    n_cube, n_grp = lax.axis_size("cube"), lax.axis_size("grp")
    rows, width = params.shape[2:]
    kept = block_ids.shape[2]
    cube_bits, grp_bits = n_cube.bit_length() - 1, n_grp.bit_length() - 1
    chunks = rows // CHUNK
    slab = jax.ShapeDtypeStruct((rows, width), F32)
    dma = pltpu.SemaphoreType.DMA
    pieces = (chunks, CHUNK, width)
    hbm = pl.BlockSpec(memory_space=pltpu.HBM)
    vmem = pl.BlockSpec(memory_space=pltpu.VMEM)
    out = pl.pallas_call(
        functools.partial(kernel, n_cube, n_grp),
        out_shape=(slab, slab, slab, jax.ShapeDtypeStruct((1, width), F32)),
        in_specs=[hbm] * 4 + [vmem],
        out_specs=(vmem,) * 4,
        scratch_shapes=[
            pltpu.VMEM((rows, width), BF16),
            pltpu.VMEM((kept, width), BF16),
            pltpu.VMEM((cube_bits * kept, width), BF16),
            pltpu.VMEM((cube_bits, 1, kept), jnp.int32),
            pltpu.VMEM(pieces, BF16),
            pltpu.VMEM(pieces, BF16),
            pltpu.VMEM(pieces, BF16),
            pltpu.VMEM(pieces, BF16),
            pltpu.VMEM((grp_bits,) + pieces, BF16),
            pltpu.VMEM(pieces, BF16),
            pltpu.VMEM(pieces, F32),
            pltpu.VMEM((8, width), F32),
            pltpu.VMEM((n_grp + 1, 8, width), F32),
            pltpu.VMEM((n_cube, 8, width), F32),
            dma((4, PIECES)),
            dma((cube_bits,)),
            dma((cube_bits,)),
            dma((cube_bits,)),
            dma((cube_bits,)),
            dma((chunks,)),
            dma((chunks,)),
            dma((chunks,)),
            dma((grp_bits, chunks)),
            dma((grp_bits, chunks)),
            dma((2, chunks)),
            dma((chunks,)),
            dma((n_grp,)),
            dma((n_grp,)),
            dma((n_cube,)),
            dma((n_cube,)),
        ],
        compiler_params=pltpu.CompilerParams(
            collective_id=0, has_side_effects=True, vmem_limit_bytes=40 * 1024 * 1024
        ),
    )(
        *(
            pltpu.with_memory_space_constraint(slab[0, 0], pltpu.HBM)
            for slab in (params, estimate, neighbour_sum, gradient)
        ),
        block_ids[0],
    )
    return (out[0][None, None], out[1][None, None], out[2][None, None], out[3][0, :1])


def solution(mesh):
    in_specs = (
        P("grp", "cube", None, None),
        P("grp", "cube", None, None),
        P("grp", "cube", None, None),
        P("grp", "cube", None, None),
        P("grp", "cube", None),
    )
    out_specs = (
        P("grp", "cube", None, None),
        P("grp", "cube", None, None),
        P("grp", "cube", None, None),
        P(),
    )
    return jax.shard_map(local, mesh=mesh, in_specs=in_specs, out_specs=out_specs, check_vma=False)
```

time: 67.8 us -> 59.6 us (0.88)
  Pallas kernels: 61.2 us -> 53 us
    pallas_call x1, Pallas kernels: 61.2 us -> 53 us  [local(): pl.pallas_call(functools.partial(kernel, n_cube, n_grp), out_shape=(slab,...]
where the time goes in v2:
time: 59.6 us; the launch traced here: 59.5 us
  Pallas kernels  53 us (89%)
  local copies, waits for them, and re-layouts  4.61 us (8%)
  between operations  1.81 us (3%)
    pallas_call x1, Pallas kernels, local(): pl.pallas_call(functools.partial(kernel, n_cube, n_grp), out_shape=(slab,...  53 us
    unnamed x5, local copies, waits for them, and re-layouts  4.61 us

profile of v2, /device:TPU:0, one launch (start us, length us, event | category | flops | bytes accessed | tf_op | source)
XLA Modules:
  0.0 59.5 jit_solution(13849372772263300577)
XLA Ops:
  0.6 0.0 copy-start
  0.6 0.6 %copy-done = s32[1,1,128]{2,1,0:T(1,128)S(1)} copy-done((s32[1,1,128]{2,1,0:T(1,128)S(1)}, s32[1,1,128]{2,1,0:T(1,128)}, u32[]{:S(2)}) %copy-start) | copy-done | bytes 536
  1.3 53.0 %shard_map.84 = (f32[4096,128]{1,0:T(8,128)S(1)}, f32[4096,128]{1,0:T(8,128)S(1)}, f32[4096,128]{1,0:T(8,128)S(1)}, f32[1,128]{1,0:T(1,128)S(1)}) custom-call(f32[4096,128]{1,0:T(8,128)} %bitcast.15, f32[4096,128]{1,0:T(8,128)} %bitcast.16, f32[4096,128]{1,0:T(8,128)} %bitcast.17, bf16[4096,128]{1,0:T(8,128)(2,1)} %bitcast.18, s32[1,128]{1,0:T(1,128)S(1)} %bitcast.13), custom_call_target="tpu_custom_call" | custom-call | tf_op jit(solution)/shard_map/pallas_call | solution.py:373
  54.3 1.3 %copy.13 = f32[1,1,4096,128]{3,2,1,0:T(8,128)} copy(f32[1,1,4096,128]{3,2,1,0:T(8,128)S(1)} %bitcast.12) | data formatting | bytes 4194304
  55.7 1.3 %copy.14 = f32[1,1,4096,128]{3,2,1,0:T(8,128)} copy(f32[1,1,4096,128]{3,2,1,0:T(8,128)S(1)} %bitcast.11) | data formatting | bytes 4194304
  57.0 1.3 %copy.15 = f32[1,1,4096,128]{3,2,1,0:T(8,128)} copy(f32[1,1,4096,128]{3,2,1,0:T(8,128)S(1)} %bitcast.10) | data formatting | bytes 4194304
Async XLA Ops:
  0.6 0.7 %copy-start = (s32[1,1,128]{2,1,0:T(1,128)S(1)}, s32[1,1,128]{2,1,0:T(1,128)}, u32[]{:S(2)}) copy-start(s32[1,1,128]{2,1,0:T(1,128)} %param.9) | copy-start | bytes 1540
